TPU v7x, 8 devices: a whole 2x2x1 slice. The times are simulated.
8 devices in a mesh: dp: 1 (over z), ep: 8 (over y, x, core).
Axes of the slice: x: 2, y: 2, z: 1, core: 2. Of those that a mesh axis runs over, the one named last changes fastest.
Arguments:
- tok_x: bfloat16 [32768, 2304], P(('dp', 'ep'))
- route_ids: int32 [32768, 2], P(('dp', 'ep'))
- route_gate: float32 [32768, 2], P(('dp', 'ep'))
- w_in: bfloat16 [8, 2304, 5760], P('ep')
- w_out: bfloat16 [8, 5760, 2304], P('ep')
- shared_in: bfloat16 [2304, 5760], replicated
- shared_out: bfloat16 [5760, 2304], replicated
Outputs:
- output: bfloat16 [32768, 2304], P(('dp', 'ep'))
All inputs are finite; a program needn't handle non-finite values.
Results may differ from a plain program's by a relative error of at most 0.00522027.
Values are sent between devices in bfloat16 or wider.
A program may use at most 1 GiB of HBM per device.

v0:
```python
import functools

import jax
import jax.numpy as jnp
from jax import lax
from jax.experimental import pallas as pl
from jax.experimental.pallas import tpu as pltpu
from jax.sharding import PartitionSpec as P


C0 = 0.7978845608028654
C1 = C0 * 0.044715
BLOCK = 256
ADD_BLOCK = 128
VMEM_BYTES = 67043328


def gelu(a):
    half = 0.5 * a
    return half + half * jnp.tanh(a * (C0 + C1 * (a * a)))


def cuts(total, step):
    return [(s, min(step, total - s)) for s in range(0, total, step)]


def ffn_kernel(parts, count_ref, *refs):
    xs, (win_hbm, wout_hbm), outs = refs[:parts], refs[parts:parts + 2], refs[parts + 2:2 * parts + 2]
    win_v, wout_v, h_v, x_v, o_v, wsem, xsem, osem = refs[2 * parts + 2:]
    ff, width = wout_v.shape
    ends = []
    total = 0
    for k in range(parts):
        total = total + count_ref[k]
        ends.append(total)
    load_in = pltpu.make_async_copy(win_hbm, win_v, wsem.at[0])
    load_out = pltpu.make_async_copy(wout_hbm, wout_v, wsem.at[1])
    load_in.start()
    load_out.start()

    def each_part(i, act):
        for k in range(parts):
            first = ends[k - 1] if k else 0

            @pl.when((i >= first) & (i < ends[k]))
            def _():
                act(k, pl.multiple_of((i - first) * BLOCK, BLOCK))

    def fetch(i, slot):
        each_part(i, lambda k, row: pltpu.make_async_copy(xs[k].at[pl.ds(row, BLOCK)], x_v.at[slot], xsem.at[slot]).start())

    def put(i, slot):
        each_part(i, lambda k, row: pltpu.make_async_copy(o_v.at[slot], outs[k].at[pl.ds(row, BLOCK)], osem.at[slot]).start())

    def wait_fetch(slot):
        pltpu.make_async_copy(xs[0].at[pl.ds(0, BLOCK)], x_v.at[slot], xsem.at[slot]).wait()

    def wait_put(slot):
        pltpu.make_async_copy(o_v.at[slot], outs[0].at[pl.ds(0, BLOCK)], osem.at[slot]).wait()

    fetch(0, 0)
    load_in.wait()

    @pl.when(total == 0)
    def _():
        load_out.wait()

    def step(i, carry):
        slot = lax.rem(i, 2)
        fetch(i + 1, 1 - slot)
        wait_fetch(slot)
        for st, sz in cuts(ff, 1280):
            a = jnp.dot(x_v[slot], win_v[:, st:st + sz], preferred_element_type=jnp.float32)
            h_v[:, st:st + sz] = gelu(a).astype(jnp.bfloat16)

        @pl.when(i == 0)
        def _():
            load_out.wait()

        @pl.when(i >= 2)
        def _():
            wait_put(slot)

        for st, sz in cuts(width, 768):
            o_v[slot, :, st:st + sz] = jnp.dot(h_v[...], wout_v[:, st:st + sz], preferred_element_type=jnp.float32).astype(jnp.bfloat16)
        put(i, slot)
        return carry

    lax.fori_loop(0, total, step, 0)

    @pl.when(total >= 1)
    def _():
        wait_put(lax.rem(total - 1, 2))

    @pl.when(total >= 2)
    def _():
        wait_put(lax.rem(total, 2))


def ffn(xs, counts, w_in, w_out):
    parts = len(xs)
    width, ff = w_in.shape
    rows = xs[0].shape[0]
    hbm = pl.BlockSpec(memory_space=pl.ANY)
    return pl.pallas_call(
        functools.partial(ffn_kernel, parts),
        in_specs=[pl.BlockSpec(memory_space=pltpu.SMEM)] + [hbm] * (parts + 2),
        out_specs=[hbm] * parts,
        out_shape=[jax.ShapeDtypeStruct((rows, width), x.dtype) for x in xs],
        scratch_shapes=[
            pltpu.VMEM((width, ff), jnp.bfloat16), pltpu.VMEM((ff, width), jnp.bfloat16), pltpu.VMEM((BLOCK, ff), jnp.bfloat16),
            pltpu.VMEM((2, BLOCK, width), jnp.bfloat16), pltpu.VMEM((2, BLOCK, width), jnp.bfloat16),
            pltpu.SemaphoreType.DMA((2,)), pltpu.SemaphoreType.DMA((2,)), pltpu.SemaphoreType.DMA((2,))],
        compiler_params=pltpu.CompilerParams(vmem_limit_bytes=VMEM_BYTES),
        cost_estimate=pl.CostEstimate(flops=2 * parts * rows * width * ff, bytes_accessed=4 * parts * rows * width + 4 * width * ff, transcendentals=0))(counts, *xs, w_in, w_out)


def add_kernel(parts, starts, final, count_ref, pair_ref, gate_ref, *refs):
    n_in = starts + 1
    ins, tables, (out,) = refs[:n_in], refs[n_in:n_in + parts], refs[n_in + parts:n_in + parts + 1]
    acc, rows_v, wide, buf_a, buf_b, rsem, asem, bsem = refs[n_in + parts + 1:]
    tokens, width = acc.shape
    block = rows_v.shape[1]
    cap = tables[0].shape[0]
    io = buf_a.shape[1]
    halves = cuts(width, (width // 256) * 128 or width)

    if starts:
        per = tokens // starts // io
        n_io = tokens // io

        def load(i):
            a = pltpu.make_async_copy(ins[0].at[pl.ds(i * io, io)], buf_a.at[i % 2], asem.at[i % 2])
            b = pltpu.make_async_copy(ins[1 + i // per].at[pl.ds((i % per) * io, io)], buf_b.at[i % 2], bsem.at[i % 2])
            return a, b

        for c in load(0):
            c.start()
        for i in range(n_io):
            if i + 1 < n_io:
                for c in load(i + 1):
                    c.start()
            for c in load(i):
                c.wait()
            acc[pl.ds(i * io, io), :] = buf_a[i % 2].astype(jnp.float32) + buf_b[i % 2].astype(jnp.float32)
    else:
        whole = pltpu.make_async_copy(ins[0], acc, asem.at[0])
        whole.start()
        whole.wait()

    for k in range(parts):
        number = count_ref[k]
        blocks = (number + block - 1) // block

        def fetch(b, slot, k=k):
            return pltpu.make_async_copy(tables[k].at[pl.ds(pl.multiple_of(b * block, block), block)], rows_v.at[slot], rsem.at[slot])

        @pl.when(blocks > 0)
        def _(fetch=fetch):
            fetch(0, 0).start()

        def one_block(b, carry, k=k, fetch=fetch, blocks=blocks, number=number):
            slot = lax.rem(b, 2)

            @pl.when(b + 1 < blocks)
            def _():
                fetch(b + 1, 1 - slot).start()

            fetch(b, slot).wait()
            wide[...] = rows_v[slot].astype(jnp.float32)
            here = jnp.minimum(block, number - b * block)

            def some_rows(r, unroll):
                pairs = [pair_ref[k * cap + b * block + r + u] for u in range(unroll)]
                toks = [lax.shift_right_logical(p, 1) for p in pairs]
                gates = [gate_ref[p] for p in pairs]
                for st, sz in halves:
                    sums = [acc[pl.ds(t, 1), st:st + sz] + g * wide[pl.ds(r + u, 1), st:st + sz] for u, (t, g) in enumerate(zip(toks, gates))]
                    for t, s in zip(toks, sums):
                        acc[pl.ds(t, 1), st:st + sz] = s

            def four(q, c):
                some_rows(q * 4, 4)
                return c

            def single(r, c):
                some_rows(r, 1)
                return c

            lax.fori_loop(0, here // 4, four, 0)
            lax.fori_loop(here // 4 * 4, here, single, 0)
            return carry

        lax.fori_loop(0, blocks, one_block, 0)

    if final:
        n_io = tokens // io

        def store(i):
            return pltpu.make_async_copy(buf_a.at[i % 2], out.at[pl.ds(i * io, io)], asem.at[i % 2])

        for i in range(n_io):
            if i >= 2:
                store(i - 2).wait()
            buf_a[i % 2] = acc[pl.ds(i * io, io), :].astype(jnp.bfloat16)
            store(i).start()
        for i in range(max(n_io - 2, 0), n_io):
            store(i).wait()
    else:
        whole = pltpu.make_async_copy(acc, out, asem.at[0])
        whole.start()
        whole.wait()


def add_rows(ins, tables, counts, pairs, gates, tokens, final, io=256):
    width = tables[0].shape[1]
    starts = len(ins) - 1
    hbm = pl.BlockSpec(memory_space=pl.ANY)
    smem = pl.BlockSpec(memory_space=pltpu.SMEM)
    return pl.pallas_call(
        functools.partial(add_kernel, len(tables), starts, final),
        in_specs=[smem] * 3 + [hbm] * (len(ins) + len(tables)),
        out_specs=hbm,
        out_shape=jax.ShapeDtypeStruct((tokens, width), jnp.bfloat16 if final else jnp.float32),
        scratch_shapes=[
            pltpu.VMEM((tokens, width), jnp.float32), pltpu.VMEM((2, ADD_BLOCK, width), jnp.bfloat16), pltpu.VMEM((ADD_BLOCK, width), jnp.float32),
            pltpu.VMEM((2, io, width), jnp.bfloat16), pltpu.VMEM((2, io, width), jnp.bfloat16),
            pltpu.SemaphoreType.DMA((2,)), pltpu.SemaphoreType.DMA((2,)), pltpu.SemaphoreType.DMA((2,))],
        compiler_params=pltpu.CompilerParams(vmem_limit_bytes=VMEM_BYTES),
        cost_estimate=pl.CostEstimate(flops=60 * 1000 * 1000 * 1000, bytes_accessed=6 * tokens * width, transcendentals=0))(counts, pairs, gates, *ins, *tables)


def after(value, *others):
    return lax.optimization_barrier((value,) + others)[0]


def solution(mesh):
    group_size = mesh.shape['ep']

    def swap(x, bits):
        return lax.ppermute(x, 'ep', [(i, i ^ bits) for i in range(group_size)])

    def layer(tok_x, route_ids, route_gate, w_in, w_out, shared_in, shared_out):
        tokens, _ = tok_x.shape
        top_k = route_ids.shape[1]
        experts = group_size
        capacity = tokens * group_size * top_k // experts
        local_cap = 2 * tokens * top_k // experts
        half = tokens // 2
        me = lax.axis_index('ep')
        partner = jnp.bitwise_xor(me, jnp.arange(experts, dtype=jnp.int32))

        flat_ids = route_ids.reshape(-1)
        onehot = (flat_ids[:, None] == jnp.arange(experts, dtype=jnp.int32)[None, :]).astype(jnp.int32)
        running = jnp.cumsum(onehot, axis=0)
        rank = jnp.sum(running * onehot, axis=1) - 1
        counts = running[-1]
        pair_number = jnp.arange(tokens * top_k, dtype=jnp.int32)
        lists = jnp.zeros((experts * local_cap,), jnp.int32).at[flat_ids * local_cap + rank].set(pair_number)
        lists = lists.reshape(experts, local_cap)
        notes = jnp.concatenate([lists, jnp.broadcast_to(jnp.pad(counts, (0, 128 - experts))[None, :], (experts, 128))], axis=1)
        notes = lax.all_to_all(notes, 'ep', 0, 0, tiled=True)
        all_counts = notes[:, local_cap:local_cap + experts]
        offset = jnp.cumsum(all_counts, axis=0) - all_counts
        kept = jnp.clip(capacity - offset, 0, all_counts)
        kept_out = lax.dynamic_index_in_dim(kept, me, 0, keepdims=False)[partner]
        kept_here = lax.dynamic_index_in_dim(kept, me, 1, keepdims=False)[partner]
        here_toks = notes[partner, :local_cap] // top_k
        home_pairs = lists[partner]
        block_counts = (kept_here + BLOCK - 1) // BLOCK
        gates = route_gate.reshape(-1)

        from_core = swap(tok_x, 1)
        from_x = swap(tok_x, 2)
        from_y = swap(tok_x, 4)

        every = jnp.full((1,), tokens // BLOCK, jnp.int32)
        shared_y, = ffn([tok_x], every, shared_in, shared_out)

        home = [None] * experts

        def expert(group, sources, previous):
            toks = after(here_toks, previous) if group == (0, 1) else here_toks
            rows = [x[toks[s]] for x, s in zip(sources, group)]
            number = after(jnp.stack([block_counts[s] for s in group]), previous)
            outs = ffn(rows, number, w_in[0], w_out[0])
            for s, out in zip(group, outs):
                home[s] = swap(out, s) if s else out
            return outs[0]

        part_x, part_y = from_x[:half], from_y[half:]
        diag_a = swap(part_x, 4)
        diag_b = swap(part_y, 2)
        core_x = swap(from_x, 1)
        core_y = swap(from_y, 1)
        last = expert((2, 4), (from_x, from_y), shared_y)
        diag_a, diag_b = after(diag_a, last), after(diag_b, last)
        diag = jnp.concatenate([diag_a, diag_b], axis=0)
        core_diag = swap(diag, 1)
        last = expert((3, 5), (core_x, core_y), last)
        last = expert((6,), (diag,), last)
        last = expert((7,), (core_diag,), last)
        last = expert((0, 1), (tok_x, from_core), last)

        def add(ins, classes, final):
            return add_rows(ins, [home[s] for s in classes], jnp.stack([kept_out[s] for s in classes]),
                            jnp.concatenate([home_pairs[s] for s in classes]), gates, tokens, final)

        total = add([tok_x, shared_y], (2, 4, 3, 5, 0, 1, 6), False)
        return add([total], (7,), True)

    row_spec = P(('dp', 'ep'), None)
    expert_spec = P('ep', None, None)
    whole_spec = P(None, None)
    return jax.shard_map(layer, mesh=mesh, in_specs=(row_spec, row_spec, row_spec, expert_spec, expert_spec, whole_spec, whole_spec), out_specs=row_spec, check_vma=False)
```

profile of v0, /device:TPU:0, one launch (start us, length us, event | category | flops | bytes accessed | tf_op | source)
XLA Modules:
  0.0 1866.7 jit_solution(10820906324053171555)
XLA Ops:
  0.0 3.3 collective-permute-start.1
  3.3 1.5 collective-permute-start
  4.8 1.4 copy.15
  6.2 1.2 eq.29
  7.4 1.2 eq.25
  10.1 1.4 mul.21
  11.6 2.4 reduce-window.6
  14.6 2.7 copy.20
  17.3 4.4 select_reduce_fusion
  21.8 30.5 %scatter_custom_fusion = s32[16384]{0:T(1024)S(1)} fusion(s32[8192]{0:T(1024)S(1)} %bitcast.80, s32[8192]{0:T(1024)S(1)} %iota.15, s32[]{:T(128)} %copy.38), kind=kCustom, calls=%fused_computation.37 | custom fusion | bytes 65540 | tf_op jit(solution)/shard_map/scatter | solution.py:259
  53.8 2.7 all-to-all-start
  57.6 271.7 %shard_map.73.refs_1_ = bf16[4096,2304]{1,0:T(8,128)(2,1)} custom-call(s32[1]{0:T(128)} %constant.65.clone.1.count_ref, bf16[4096,2304]{1,0:T(8,128)(2,1)} %refs_0_.3, bf16[2304,5760]{1,0:T(8,128)(2,1)} %refs_1_.1, bf16[5760,2304]{1,0:T(8,128)(2,1)} %refs_2_.1), custom_call_target="tpu_custom_call" | custom-call | flops 108716359680 | bytes 90832896 | tf_op jit(solution)/shard_map/pallas_call | solution.py:105
  329.9 81.0 %all-to-all-done = s32[8,1,2176]{2,1,0:T(1,128)} async-done(((s32[8,1,2176]{2,1,0:T(1,128)}), s32[8,1,2176]{2,1,0:T(1,128)}, u32[]{:S(2)}, u32[]{:S(2)}) %all-to-all-start) | async-done | bytes 69664 | tf_op jit(solution)/shard_map/all_to_all | solution.py:262
  413.9 1.8 pad_add_fusion.count_ref
  416.3 31.5 %while.2 = (s32[]{:T(128)}, s32[8,2176]{1,0:T(8,128)S(1)}, s32[8,2]{0,1:T(2,128)}, s32[8,2048]{1,0:T(8,128)}) while((s32[]{:T(128)}, s32[8,2176]{1,0:T(8,128)S(1)}, s32[8,2]{0,1:T(2,128)}, s32[8,2048]{1,0:T(8,128)}) %tuple.66), condition=%wide.while_cond.clone, body=%wide.while_body.sunk.clone | while | flops 2 | bytes 32873 | solution.py:268
  417.5 1.2 dynamic-slice.9
  418.7 1.5 dynamic-update-slice.22
  421.4 1.2 dynamic-slice.9
  422.6 1.5 dynamic-update-slice.22
  425.3 1.2 dynamic-slice.9
  426.6 1.5 dynamic-update-slice.22
  429.3 1.2 dynamic-slice.9
  430.5 1.5 dynamic-update-slice.22
  433.2 1.2 dynamic-slice.9
  434.4 1.5 dynamic-update-slice.22
  437.2 1.2 dynamic-slice.9
  438.4 1.5 dynamic-update-slice.22
  441.1 1.2 dynamic-slice.9
  442.3 1.5 dynamic-update-slice.22
  445.0 1.2 dynamic-slice.9
  446.2 1.5 dynamic-update-slice.22
  449.9 8.0 slice.193
  457.9 1.6 collective-permute-start.9
  459.5 7.9 slice.192
  467.4 1.4 collective-permute-start.8
  468.8 27.0 %gather_fusion.4 = bf16[2048,2304]{1,0:T(8,128)(2,1)} fusion(bf16[4096,2304]{1,0:T(8,128)(2,1)} %collective-permute-done.1, s32[2048]{0:T(1024)S(1)} %broadcast_clamp_fusion.6), kind=kCustom, calls=%fused_computation.4 | custom fusion | bytes 18882560 | tf_op jit(solution)/shard_map/gather | solution.py:284
  495.8 27.0 %gather_fusion.3 = bf16[2048,2304]{1,0:T(8,128)(2,1)} fusion(bf16[4096,2304]{1,0:T(8,128)(2,1)} %collective-permute-done, s32[2048]{0:T(1024)S(1)} %broadcast_clamp_fusion.7), kind=kCustom, calls=%fused_computation.3 | custom fusion | bytes 18882560 | tf_op jit(solution)/shard_map/gather | solution.py:284
  522.8 129.4 %shard_map.74 = (bf16[2048,2304]{1,0:T(8,128)(2,1)}, bf16[2048,2304]{1,0:T(8,128)(2,1)}) custom-call(s32[2]{0:T(128)} %pad_add_fusion.count_ref, bf16[2048,2304]{1,0:T(8,128)(2,1)} %gather_fusion.3, bf16[2048,2304]{1,0:T(8,128)(2,1)} %gather_fusion.4, bf16[2304,5760]{1,0:T(8,128)(2,1)} %bitcast.100, bf16[5760,2304]{1,0:T(8,128)(2,1)} %bitcast.105), custom_call_target="tpu_custom_call" | custom-call | flops 108716359680 | bytes 90832896 | tf_op jit(solution)/shard_map/pallas_call | solution.py:105
  652.3 10.8 collective-permute-done.9
  663.1 9.2 collective-permute-done.8
  672.3 7.8 constant_dynamic-update-slice_fusion.3
  680.2 8.0 constant_dynamic-update-slice_fusion.1
  688.7 1.8 pad_add_fusion.1.count_ref
  691.6 27.2 %gather_fusion.7 = bf16[2048,2304]{1,0:T(8,128)(2,1)} fusion(bf16[4096,2304]{1,0:T(8,128)(2,1)} %constant_dynamic-update-slice_fusion.1, s32[2048]{0:T(1024)S(1)} %broadcast_clamp_fusion.3), kind=kCustom, calls=%fused_computation.7 | custom fusion | bytes 18882560 | tf_op jit(solution)/shard_map/gather | solution.py:284
  718.7 27.3 %collective-permute-start.3 = (bf16[2048,2304]{1,0:T(8,128)(2,1)}, bf16[2048,2304]{1,0:T(8,128)(2,1)}, u32[]{:S(2)}, u32[]{:S(2)}) collective-permute-start(bf16[2048,2304]{1,0:T(8,128)(2,1)} %get-tuple-element.21), channel_id=1, source_target_pairs={{0,4},{1,5},{2,6},{3,7},{4,0},{5,1},{6,2},{7,3}} | collective-permute-start | bytes 28311560 | tf_op jit(solution)/shard_map/ppermute | solution.py:241
  746.0 27.0 %gather_fusion.6 = bf16[2048,2304]{1,0:T(8,128)(2,1)} fusion(bf16[4096,2304]{1,0:T(8,128)(2,1)} %collective-permute-done.5, s32[2048]{0:T(1024)S(1)} %broadcast_clamp_fusion.4), kind=kCustom, calls=%fused_computation.6 | custom fusion | bytes 18882560 | tf_op jit(solution)/shard_map/gather | solution.py:284
  773.0 27.0 %gather_fusion.5 = bf16[2048,2304]{1,0:T(8,128)(2,1)} fusion(bf16[4096,2304]{1,0:T(8,128)(2,1)} %collective-permute-done.4, s32[2048]{0:T(1024)S(1)} %broadcast_clamp_fusion.5), kind=kCustom, calls=%fused_computation.5 | custom fusion | bytes 18882560 | tf_op jit(solution)/shard_map/gather | solution.py:284
  800.1 65.9 %shard_map.75 = (bf16[2048,2304]{1,0:T(8,128)(2,1)}, bf16[2048,2304]{1,0:T(8,128)(2,1)}) custom-call(s32[2]{0:T(128)} %pad_add_fusion.1.count_ref, bf16[2048,2304]{1,0:T(8,128)(2,1)} %gather_fusion.5, bf16[2048,2304]{1,0:T(8,128)(2,1)} %gather_fusion.6, bf16[2304,5760]{1,0:T(8,128)(2,1)} %bitcast.101, bf16[5760,2304]{1,0:T(8,128)(2,1)} %bitcast.106), custom_call_target="tpu_custom_call" | custom-call | flops 108716359680 | bytes 90832896 | tf_op jit(solution)/shard_map/pallas_call | solution.py:105
  866.0 81.8 %shard_map.76 = bf16[2048,2304]{1,0:T(8,128)(2,1)} custom-call(s32[1]{0:T(128)} %get-tuple-element.25.count_ref, bf16[2048,2304]{1,0:T(8,128)(2,1)} %gather_fusion.7, bf16[2304,5760]{1,0:T(8,128)(2,1)} %bitcast.102, bf16[5760,2304]{1,0:T(8,128)(2,1)} %bitcast.107), custom_call_target="tpu_custom_call" | custom-call | flops 54358179840 | bytes 71958528 | tf_op jit(solution)/shard_map/pallas_call | solution.py:105
  947.8 206.1 %collective-permute-start.13 = (bf16[2048,2304]{1,0:T(8,128)(2,1)}, bf16[2048,2304]{1,0:T(8,128)(2,1)}, u32[]{:S(2)}, u32[]{:S(2)}) collective-permute-start(bf16[2048,2304]{1,0:T(8,128)(2,1)} %shard_map.76), channel_id=1, source_target_pairs={{0,6},{1,7},{2,4},{3,5},{4,2},{5,3},{6,0},{7,1}} | collective-permute-start | bytes 28311560 | tf_op jit(solution)/shard_map/ppermute | solution.py:241
  1153.8 27.1 %gather_fusion.8 = bf16[2048,2304]{1,0:T(8,128)(2,1)} fusion(bf16[4096,2304]{1,0:T(8,128)(2,1)} %collective-permute-done.10, s32[2048]{0:T(1024)} %broadcast_clamp_fusion.2), kind=kCustom, calls=%fused_computation.8 | custom fusion | bytes 18882560 | tf_op jit(solution)/shard_map/gather | solution.py:284
  1181.0 81.8 %shard_map.77 = bf16[2048,2304]{1,0:T(8,128)(2,1)} custom-call(s32[1]{0:T(128)} %get-tuple-element.28.count_ref, bf16[2048,2304]{1,0:T(8,128)(2,1)} %gather_fusion.8, bf16[2304,5760]{1,0:T(8,128)(2,1)} %bitcast.103, bf16[5760,2304]{1,0:T(8,128)(2,1)} %bitcast.108), custom_call_target="tpu_custom_call" | custom-call | flops 54358179840 | bytes 71958528 | tf_op jit(solution)/shard_map/pallas_call | solution.py:105
  1262.8 0.9 compare_select_fusion.1
  1263.8 27.0 %gather_fusion.9 = bf16[2048,2304]{1,0:T(8,128)(2,1)} fusion(bf16[4096,2304]{1,0:T(8,128)(2,1)} %refs_0_.3, s32[2048]{0:T(1024)S(1)} %get-tuple-element.80), kind=kCustom, calls=%fused_computation.9 | custom fusion | bytes 18882560 | tf_op jit(solution)/shard_map/gather | solution.py:284
  1290.8 32.1 %collective-permute-start.7 = (bf16[2048,2304]{1,0:T(8,128)(2,1)}, bf16[2048,2304]{1,0:T(8,128)(2,1)}, u32[]{:S(2)}, u32[]{:S(2)}) collective-permute-start(bf16[2048,2304]{1,0:T(8,128)(2,1)} %get-tuple-element.24), channel_id=1, source_target_pairs={{0,5},{1,4},{2,7},{3,6},{4,1},{5,0},{6,3},{7,2}} | collective-permute-start | bytes 28311560 | tf_op jit(solution)/shard_map/ppermute | solution.py:241
  1322.9 27.0 %gather_fusion.10 = bf16[2048,2304]{1,0:T(8,128)(2,1)} fusion(bf16[4096,2304]{1,0:T(8,128)(2,1)} %collective-permute-done.11, s32[2048]{0:T(1024)S(1)} %get-tuple-element.79), kind=kCustom, calls=%fused_computation.10 | custom fusion | bytes 18882560 | tf_op jit(solution)/shard_map/gather | solution.py:284
  1349.9 113.5 %shard_map.78 = (bf16[2048,2304]{1,0:T(8,128)(2,1)}, bf16[2048,2304]{1,0:T(8,128)(2,1)}) custom-call(s32[2]{0:T(128)} %bitcast.97, bf16[2048,2304]{1,0:T(8,128)(2,1)} %gather_fusion.9, bf16[2048,2304]{1,0:T(8,128)(2,1)} %gather_fusion.10, bf16[2304,5760]{1,0:T(8,128)(2,1)} %bitcast.104, bf16[5760,2304]{1,0:T(8,128)(2,1)} %bitcast.109), custom_call_target="tpu_custom_call" | custom-call | flops 108716359680 | bytes 90832896 | tf_op jit(solution)/shard_map/pallas_call | solution.py:105
  1463.5 1.6 gather_fusion.1
  1465.1 1.4 copy.19
  1466.5 1.8 reshape.302.gate_ref
  1471.7 3.7 stack.12.count_ref
  1475.4 239.5 %collective-permute-done.7.refs_5_ = bf16[2048,2304]{1,0:T(8,128)(2,1)} collective-permute-done((bf16[2048,2304]{1,0:T(8,128)(2,1)}, bf16[2048,2304]{1,0:T(8,128)(2,1)}, u32[]{:S(2)}, u32[]{:S(2)}) %collective-permute-start.7) | collective-permute-done | bytes 9437216 | tf_op jit(solution)/shard_map/ppermute | solution.py:241
  1714.9 114.6 %shard_map.79.refs_0_ = f32[4096,2304]{1,0:T(8,128)} custom-call(s32[7]{0:T(128)} %stack.12.count_ref, s32[14336]{0:T(1024)} %copy-done.9, f32[8192]{0:T(1024)} %reshape.302.gate_ref, bf16[4096,2304]{1,0:T(8,128)(2,1)} %refs_0_.3, bf16[4096,2304]{1,0:T(8,128)(2,1)} %shard_map.73.refs_1_, bf16[2048,2304]{1,0:T(8,128)(2,1)} %collective-permute-done.2.refs_2_, ...), custom_call_target="tpu_custom_call" | custom-call | flops 60000002048 | bytes 56623104 | tf_op jit(solution)/shard_map/pallas_call | solution.py:220
  1829.5 37.0 %shard_map.80 = bf16[4096,2304]{1,0:T(8,128)(2,1)} custom-call(s32[1]{0:T(128)} %get-tuple-element.78.count_ref, s32[2048]{0:T(1024)} %bitcast.99, f32[8192]{0:T(1024)} %reshape.302.gate_ref, f32[4096,2304]{1,0:T(8,128)} %shard_map.79.refs_0_, bf16[2048,2304]{1,0:T(8,128)(2,1)} %collective-permute-done.14.refs_1_), custom_call_target="tpu_custom_call" | custom-call | flops 60000002048 | bytes 56623104 | tf_op jit(solution)/shard_map/pallas_call | solution.py:220
  (103 shorter events, 25.7 us)
Async XLA Ops:
  0.0 415.7 %collective-permute-start.1 = (bf16[4096,2304]{1,0:T(8,128)(2,1)}, bf16[4096,2304]{1,0:T(8,128)(2,1)}, u32[]{:S(2)}, u32[]{:S(2)}) collective-permute-start(bf16[4096,2304]{1,0:T(8,128)(2,1)} %refs_0_.3), channel_id=1, source_target_pairs={{0,4},{1,5},{2,6},{3,7},{4,0},{5,1},{6,2},{7,3}} | collective-permute-start | bytes 56623112 | tf_op jit(solution)/shard_map/ppermute | solution.py:241
  3.3 412.4 %collective-permute-start = (bf16[4096,2304]{1,0:T(8,128)(2,1)}, bf16[4096,2304]{1,0:T(8,128)(2,1)}, u32[]{:S(2)}, u32[]{:S(2)}) collective-permute-start(bf16[4096,2304]{1,0:T(8,128)(2,1)} %refs_0_.3), channel_id=1, source_target_pairs={{0,2},{1,3},{2,0},{3,1},{4,6},{5,7},{6,4},{7,5}} | collective-permute-start | bytes 56623112 | tf_op jit(solution)/shard_map/ppermute | solution.py:241
  52.4 0.7 copy-start
  53.8 357.1 %all-to-all-start = ((s32[8,1,2176]{2,1,0:T(1,128)}), s32[8,1,2176]{2,1,0:T(1,128)}, u32[]{:S(2)}, u32[]{:S(2)}) async-start(s32[8,1,2176]{2,1,0:T(1,128)} %copy.18), calls=%async_computation | async-start | bytes 139264 | tf_op jit(solution)/shard_map/all_to_all | solution.py:262
  329.9 128.0 %copy-start.8 = (s32[1024]{0:T(1024)}, s32[1024]{0:T(1024)S(1)}, u32[]{:S(2)}) copy-start(s32[1024]{0:T(1024)S(1)} %pad_clamp_fusion) | copy-start | bytes 12292
  411.9 4.4 copy-start.7
  412.7 0.6 copy-start.6
  415.7 303.0 %collective-permute-start.5 = (bf16[4096,2304]{1,0:T(8,128)(2,1)}, bf16[4096,2304]{1,0:T(8,128)(2,1)}, u32[]{:S(2)}, u32[]{:S(2)}) collective-permute-start(bf16[4096,2304]{1,0:T(8,128)(2,1)} %collective-permute-done.1), channel_id=1, source_target_pairs={{0,1},{1,0},{2,3},{3,2},{4,5},{5,4},{6,7},{7,6}} | collective-permute-start | bytes 56623112 | tf_op jit(solution)/shard_map/ppermute | solution.py:241
  415.8 357.3 %collective-permute-start.4 = (bf16[4096,2304]{1,0:T(8,128)(2,1)}, bf16[4096,2304]{1,0:T(8,128)(2,1)}, u32[]{:S(2)}, u32[]{:S(2)}) collective-permute-start(bf16[4096,2304]{1,0:T(8,128)(2,1)} %collective-permute-done), channel_id=1, source_target_pairs={{0,1},{1,0},{2,3},{3,2},{4,5},{5,4},{6,7},{7,6}} | collective-permute-start | bytes 56623112 | tf_op jit(solution)/shard_map/ppermute | solution.py:241
  448.6 0.6 copy-start.1
  457.9 205.2 %collective-permute-start.9 = (bf16[2048,2304]{1,0:T(8,128)(2,1)}, bf16[2048,2304]{1,0:T(8,128)(2,1)}, u32[]{:S(2)}, u32[]{:S(2)}) collective-permute-start(bf16[2048,2304]{1,0:T(8,128)(2,1)} %slice.193), channel_id=1, source_target_pairs={{0,2},{1,3},{2,0},{3,1},{4,6},{5,7},{6,4},{7,5}} | collective-permute-start | bytes 28311560 | tf_op jit(solution)/shard_map/ppermute | solution.py:241
  467.4 204.9 %collective-permute-start.8 = (bf16[2048,2304]{1,0:T(8,128)(2,1)}, bf16[2048,2304]{1,0:T(8,128)(2,1)}, u32[]{:S(2)}, u32[]{:S(2)}) collective-permute-start(bf16[2048,2304]{1,0:T(8,128)(2,1)} %slice.192), channel_id=1, source_target_pairs={{0,4},{1,5},{2,6},{3,7},{4,0},{5,1},{6,2},{7,3}} | collective-permute-start | bytes 28311560 | tf_op jit(solution)/shard_map/ppermute | solution.py:241
  680.2 10.3 copy-start.5
  680.2 10.9 copy-start.4
  680.2 10.9 copy-start.3
  680.2 10.9 copy-start.2
  688.2 465.7 %collective-permute-start.10 = (bf16[4096,2304]{1,0:T(8,128)(2,1)}, bf16[4096,2304]{1,0:T(8,128)(2,1)}, u32[]{:S(2)}, u32[]{:S(2)}) collective-permute-start(bf16[4096,2304]{1,0:T(8,128)(2,1)} %constant_dynamic-update-slice_fusion.1), channel_id=1, source_target_pairs={{0,1},{1,0},{2,3},{3,2},{4,5},{5,4},{6,7},{7,6}} | collective-permute-start | bytes 56623112 | tf_op jit(solution)/shard_map/ppermute | solution.py:241
  688.2 602.6 %collective-permute-start.11 = (bf16[4096,2304]{1,0:T(8,128)(2,1)}, bf16[4096,2304]{1,0:T(8,128)(2,1)}, u32[]{:S(2)}, u32[]{:S(2)}) collective-permute-start(bf16[4096,2304]{1,0:T(8,128)(2,1)} %refs_0_.3), channel_id=1, source_target_pairs={{0,1},{1,0},{2,3},{3,2},{4,5},{5,4},{6,7},{7,6}} | collective-permute-start | bytes 56623112 | tf_op jit(solution)/shard_map/ppermute | solution.py:241
  691.1 772.4 %collective-permute-start.2 = (bf16[2048,2304]{1,0:T(8,128)(2,1)}, bf16[2048,2304]{1,0:T(8,128)(2,1)}, u32[]{:S(2)}, u32[]{:S(2)}) collective-permute-start(bf16[2048,2304]{1,0:T(8,128)(2,1)} %get-tuple-element.20), channel_id=1, source_target_pairs={{0,2},{1,3},{2,0},{3,1},{4,6},{5,7},{6,4},{7,5}} | collective-permute-start | bytes 28311560 | tf_op jit(solution)/shard_map/ppermute | solution.py:241
  718.7 744.7 %collective-permute-start.3 = (bf16[2048,2304]{1,0:T(8,128)(2,1)}, bf16[2048,2304]{1,0:T(8,128)(2,1)}, u32[]{:S(2)}, u32[]{:S(2)}) collective-permute-start(bf16[2048,2304]{1,0:T(8,128)(2,1)} %get-tuple-element.21), channel_id=1, source_target_pairs={{0,4},{1,5},{2,6},{3,7},{4,0},{5,1},{6,2},{7,3}} | collective-permute-start | bytes 28311560 | tf_op jit(solution)/shard_map/ppermute | solution.py:241
  947.8 527.7 %collective-permute-start.13 = (bf16[2048,2304]{1,0:T(8,128)(2,1)}, bf16[2048,2304]{1,0:T(8,128)(2,1)}, u32[]{:S(2)}, u32[]{:S(2)}) collective-permute-start(bf16[2048,2304]{1,0:T(8,128)(2,1)} %shard_map.76), channel_id=1, source_target_pairs={{0,6},{1,7},{2,4},{3,5},{4,2},{5,3},{6,0},{7,1}} | collective-permute-start | bytes 28311560 | tf_op jit(solution)/shard_map/ppermute | solution.py:241
  1153.8 561.1 %collective-permute-start.6 = (bf16[2048,2304]{1,0:T(8,128)(2,1)}, bf16[2048,2304]{1,0:T(8,128)(2,1)}, u32[]{:S(2)}, u32[]{:S(2)}) collective-permute-start(bf16[2048,2304]{1,0:T(8,128)(2,1)} %get-tuple-element.23), channel_id=1, source_target_pairs={{0,3},{1,2},{2,1},{3,0},{4,7},{5,6},{6,5},{7,4}} | collective-permute-start | bytes 28311560 | tf_op jit(solution)/shard_map/ppermute | solution.py:241
  1290.8 424.1 %collective-permute-start.7 = (bf16[2048,2304]{1,0:T(8,128)(2,1)}, bf16[2048,2304]{1,0:T(8,128)(2,1)}, u32[]{:S(2)}, u32[]{:S(2)}) collective-permute-start(bf16[2048,2304]{1,0:T(8,128)(2,1)} %get-tuple-element.24), channel_id=1, source_target_pairs={{0,5},{1,4},{2,7},{3,6},{4,1},{5,0},{6,3},{7,2}} | collective-permute-start | bytes 28311560 | tf_op jit(solution)/shard_map/ppermute | solution.py:241
  1463.4 251.4 %collective-permute-start.12 = (bf16[2048,2304]{1,0:T(8,128)(2,1)}, bf16[2048,2304]{1,0:T(8,128)(2,1)}, u32[]{:S(2)}, u32[]{:S(2)}) collective-permute-start(bf16[2048,2304]{1,0:T(8,128)(2,1)} %get-tuple-element.32), channel_id=1, source_target_pairs={{0,1},{1,0},{2,3},{3,2},{4,5},{5,4},{6,7},{7,6}} | collective-permute-start | bytes 28311560 | tf_op jit(solution)/shard_map/ppermute | solution.py:241
  1463.5 366.0 %collective-permute-start.14 = (bf16[2048,2304]{1,0:T(8,128)(2,1)}, bf16[2048,2304]{1,0:T(8,128)(2,1)}, u32[]{:S(2)}, u32[]{:S(2)}) collective-permute-start(bf16[2048,2304]{1,0:T(8,128)(2,1)} %shard_map.77), channel_id=1, source_target_pairs={{0,7},{1,6},{2,5},{3,4},{4,3},{5,2},{6,1},{7,0}} | collective-permute-start | bytes 28311560 | tf_op jit(solution)/shard_map/ppermute | solution.py:241
  1469.0 0.6 copy-start.9
where the time goes:
time: 1870 us
  Pallas kernels  896 us (48%)
  waiting for transfers between devices  341 us (18%)
  local copies, waits for them, and re-layouts  336 us (18%)
  starting transfers between devices  277 us (15%)
    pallas_call x6, Pallas kernels, ffn(): pl.pallas_call(functools.partial(ffn_kernel, parts), in_specs=[pl.BlockSp...  744 us
    ppermute x15, starting transfers between devices, swap(): return lax.ppermute(x, 'ep', [(i, i ^ bits) for i in range(group_size)])  275 us
    ppermute x15, waiting for transfers between devices, swap(): return lax.ppermute(x, 'ep', [(i, i ^ bits) for i in range(group_size)])  260 us
    gather x8, local copies, waits for them, and re-layouts, expert(): rows = [x[toks[s]] for x, s in zip(sources, group)]  216 us
    pallas_call x2, Pallas kernels, add_rows(): pl.pallas_call(functools.partial(add_kernel, len(tables), starts, final),...  152 us
    all_to_all x1, waiting for transfers between devices, layer(): notes = lax.all_to_all(notes, 'ep', 0, 0, tiled=True)  81 us
  transfers between devices with their start and end apart: 16, of which 4 were waited for; matrix products, arithmetic and copies ran while one was open for 19% of the time, Pallas kernels for 46%

commit v1 on v0

--- a/solution.py
+++ b/solution.py
@@ -24,7 +24,7 @@
     return [(s, min(step, total - s)) for s in range(0, total, step)]
 
 
-def ffn_kernel(parts, count_ref, *refs):
+def ffn_kernel(parts, base, count_ref, *refs):
     xs, (win_hbm, wout_hbm), outs = refs[:parts], refs[parts:parts + 2], refs[parts + 2:2 * parts + 2]
     win_v, wout_v, h_v, x_v, o_v, wsem, xsem, osem = refs[2 * parts + 2:]
     ff, width = wout_v.shape
@@ -47,7 +47,7 @@
                 act(k, pl.multiple_of((i - first) * BLOCK, BLOCK))
 
     def fetch(i, slot):
-        each_part(i, lambda k, row: pltpu.make_async_copy(xs[k].at[pl.ds(row, BLOCK)], x_v.at[slot], xsem.at[slot]).start())
+        each_part(i, lambda k, row: pltpu.make_async_copy(xs[k].at[pl.ds(base + row, BLOCK)], x_v.at[slot], xsem.at[slot]).start())
 
     def put(i, slot):
         each_part(i, lambda k, row: pltpu.make_async_copy(o_v.at[slot], outs[k].at[pl.ds(row, BLOCK)], osem.at[slot]).start())
@@ -97,13 +97,13 @@
         wait_put(lax.rem(total, 2))
 
 
-def ffn(xs, counts, w_in, w_out):
+def ffn(xs, counts, w_in, w_out, base=0, rows=None):
     parts = len(xs)
     width, ff = w_in.shape
-    rows = xs[0].shape[0]
+    rows = rows or xs[0].shape[0]
     hbm = pl.BlockSpec(memory_space=pl.ANY)
     return pl.pallas_call(
-        functools.partial(ffn_kernel, parts),
+        functools.partial(ffn_kernel, parts, base),
         in_specs=[pl.BlockSpec(memory_space=pltpu.SMEM)] + [hbm] * (parts + 2),
         out_specs=[hbm] * parts,
         out_shape=[jax.ShapeDtypeStruct((rows, width), x.dtype) for x in xs],
@@ -126,12 +126,12 @@
     halves = cuts(width, (width // 256) * 128 or width)
 
     if starts:
-        per = tokens // starts // io
+        place = [(k, r) for k in range(starts) for r in range(0, ins[1 + k].shape[0], io)]
         n_io = tokens // io
 
         def load(i):
             a = pltpu.make_async_copy(ins[0].at[pl.ds(i * io, io)], buf_a.at[i % 2], asem.at[i % 2])
-            b = pltpu.make_async_copy(ins[1 + i // per].at[pl.ds((i % per) * io, io)], buf_b.at[i % 2], bsem.at[i % 2])
+            b = pltpu.make_async_copy(ins[1 + place[i][0]].at[pl.ds(place[i][1], io)], buf_b.at[i % 2], bsem.at[i % 2])
             return a, b
 
         for c in load(0):
@@ -259,55 +259,65 @@
         lists = jnp.zeros((experts * local_cap,), jnp.int32).at[flat_ids * local_cap + rank].set(pair_number)
         lists = lists.reshape(experts, local_cap)
         notes = jnp.concatenate([lists, jnp.broadcast_to(jnp.pad(counts, (0, 128 - experts))[None, :], (experts, 128))], axis=1)
+        core_note = lax.dynamic_index_in_dim(notes, jnp.bitwise_xor(me, 1), 0, keepdims=True)
+        core_note = swap(core_note, 1)[0]
         notes = lax.all_to_all(notes, 'ep', 0, 0, tiled=True)
+        home_pairs = lists[partner]
+        gates = route_gate.reshape(-1)
+
+        from_core = swap(tok_x, 1)
+        from_x = swap(tok_x, 2)
+        from_y = swap(tok_x, 4)
+
+        home = [None] * experts
+
+        def expert(group, sources, previous, toks, numbers):
+            rows = [x[toks[s]] for x, s in zip(sources, group)]
+            number = after(jnp.stack([numbers[s] for s in group]), previous)
+            outs = ffn(rows, number, w_in[0], w_out[0])
+            for s, out in zip(group, outs):
+                home[s] = swap(out, s) if s else out
+            return outs[0]
+
+        own_list = lax.dynamic_index_in_dim(lists, me, 0, keepdims=False)
+        own_count = lax.dynamic_index_in_dim(counts, me, 0, keepdims=False)
+        core_count = lax.dynamic_index_in_dim(core_note, local_cap + me, 0, keepdims=False)
+        core_toks = (own_list // top_k, core_note[:local_cap] // top_k)
+        core_numbers = ((own_count + BLOCK - 1) // BLOCK, (core_count + BLOCK - 1) // BLOCK)
+        first_rows = tokens * 3 // 8
+        rest_rows = tokens - first_rows
+        last = expert((0, 1), (tok_x, from_core), counts, core_toks, core_numbers)
+        shared_a, = ffn([tok_x], after(jnp.full((1,), first_rows // BLOCK, jnp.int32), last), shared_in, shared_out, 0, first_rows)
+        from_x, from_y, notes = lax.optimization_barrier((from_x, from_y, notes, shared_a))[:3]
+
         all_counts = notes[:, local_cap:local_cap + experts]
         offset = jnp.cumsum(all_counts, axis=0) - all_counts
         kept = jnp.clip(capacity - offset, 0, all_counts)
         kept_out = lax.dynamic_index_in_dim(kept, me, 0, keepdims=False)[partner]
         kept_here = lax.dynamic_index_in_dim(kept, me, 1, keepdims=False)[partner]
-        here_toks = notes[partner, :local_cap] // top_k
-        home_pairs = lists[partner]
+        here_toks = notes[partner][:, :local_cap] // top_k
         block_counts = (kept_here + BLOCK - 1) // BLOCK
-        gates = route_gate.reshape(-1)
-
-        from_core = swap(tok_x, 1)
-        from_x = swap(tok_x, 2)
-        from_y = swap(tok_x, 4)
-
-        every = jnp.full((1,), tokens // BLOCK, jnp.int32)
-        shared_y, = ffn([tok_x], every, shared_in, shared_out)
-
-        home = [None] * experts
-
-        def expert(group, sources, previous):
-            toks = after(here_toks, previous) if group == (0, 1) else here_toks
-            rows = [x[toks[s]] for x, s in zip(sources, group)]
-            number = after(jnp.stack([block_counts[s] for s in group]), previous)
-            outs = ffn(rows, number, w_in[0], w_out[0])
-            for s, out in zip(group, outs):
-                home[s] = swap(out, s) if s else out
-            return outs[0]
 
         part_x, part_y = from_x[:half], from_y[half:]
         diag_a = swap(part_x, 4)
         diag_b = swap(part_y, 2)
         core_x = swap(from_x, 1)
         core_y = swap(from_y, 1)
-        last = expert((2, 4), (from_x, from_y), shared_y)
+        last = expert((2, 4), (from_x, from_y), shared_a, here_toks, block_counts)
         diag_a, diag_b = after(diag_a, last), after(diag_b, last)
         diag = jnp.concatenate([diag_a, diag_b], axis=0)
         core_diag = swap(diag, 1)
-        last = expert((3, 5), (core_x, core_y), last)
-        last = expert((6,), (diag,), last)
-        last = expert((7,), (core_diag,), last)
-        last = expert((0, 1), (tok_x, from_core), last)
+        last = expert((3, 5), (core_x, core_y), last, here_toks, block_counts)
+        last = expert((6,), (diag,), last, here_toks, block_counts)
+        last = expert((7,), (core_diag,), last, here_toks, block_counts)
+        shared_b, = ffn([tok_x], after(jnp.full((1,), rest_rows // BLOCK, jnp.int32), last), shared_in, shared_out, first_rows, rest_rows)
 
         def add(ins, classes, final):
             return add_rows(ins, [home[s] for s in classes], jnp.stack([kept_out[s] for s in classes]),
                             jnp.concatenate([home_pairs[s] for s in classes]), gates, tokens, final)
 
-        total = add([tok_x, shared_y], (2, 4, 3, 5, 0, 1, 6), False)
-        return add([total], (7,), True)
+        total = add([tok_x, shared_a, shared_b], (0, 1, 2, 4), False)
+        return add([total], (3, 5, 6, 7), True)
 
     row_spec = P(('dp', 'ep'), None)
     expert_spec = P('ep', None, None)

time: 1870 us -> 2200 us (1.18)
  waiting for transfers between devices: 341 us -> 561 us
  starting transfers between devices: 277 us -> 397 us
  local copies, waits for them, and re-layouts: 336 us -> 298 us
    all_to_all x1, waiting for transfers between devices: 81 us -> 321 us  [layer(): notes = lax.all_to_all(notes, 'ep', 0, 0, tiled=True)]
    ppermute x15 -> x16, starting transfers between devices: 275 us -> 394 us  [swap(): return lax.ppermute(x, 'ep', [(i, i ^ bits) for i in range(group_size)])]
    gather x32 -> x1, local copies, waits for them, and re-layouts: 31.4 us -> 0.58 us  [layer(): here_toks = notes[partner][:, :local_cap] // top_k]
    ppermute x15 -> x16, waiting for transfers between devices: 260 us -> 240 us  [swap(): return lax.ppermute(x, 'ep', [(i, i ^ bits) for i in range(group_size)])]
    pallas_call x6 -> x7, Pallas kernels: 744 us -> 762 us  [ffn(): pl.pallas_call(functools.partial(ffn_kernel, parts, base), in_specs=[pl.B...]
  transfers between devices with their start and end apart: 16 -> 17, of which waited for: 4 -> 3; matrix products, arithmetic and copies ran while one was open for 19% -> 14% of each run, Pallas kernels for 46% -> 38%
where the time goes in v1:
time: 2200 us; the launch traced here: 2190 us
  Pallas kernels  913 us (42%)
  waiting for transfers between devices  561 us (26%)
  starting transfers between devices  397 us (18%)
  local copies, waits for them, and re-layouts  298 us (14%)
    pallas_call x7, Pallas kernels, ffn(): pl.pallas_call(functools.partial(ffn_kernel, parts, base), in_specs=[pl.B...  762 us
    ppermute x16, starting transfers between devices, swap(): return lax.ppermute(x, 'ep', [(i, i ^ bits) for i in range(group_size)])  394 us
    all_to_all x1, waiting for transfers between devices, layer(): notes = lax.all_to_all(notes, 'ep', 0, 0, tiled=True)  321 us
    ppermute x16, waiting for transfers between devices, swap(): return lax.ppermute(x, 'ep', [(i, i ^ bits) for i in range(group_size)])  240 us
    gather x8, local copies, waits for them, and re-layouts, expert(): rows = [x[toks[s]] for x, s in zip(sources, group)]  216 us
    pallas_call x2, Pallas kernels, add_rows(): pl.pallas_call(functools.partial(add_kernel, len(tables), starts, final),...  151 us
  transfers between devices with their start and end apart: 17, of which 3 were waited for; matrix products, arithmetic and copies ran while one was open for 14% of the time, Pallas kernels for 38%

profile of v1, /device:TPU:0, one launch (start us, length us, event | category | flops | bytes accessed | tf_op | source)
XLA Modules:
  0.0 2191.5 jit_solution(16521729483423641534)
XLA Ops:
  0.0 0.8 collective-permute-start.3
  0.8 2.5 collective-permute-start.1
  3.3 1.5 collective-permute-start
  4.8 1.4 copy.15
  6.2 1.2 eq.29
  7.4 1.2 eq.25
  8.6 0.8 broadcast_multiply_fusion
  9.4 0.6 copy.14
  10.1 1.4 mul.21
  11.6 2.4 reduce-window.6
  14.7 2.7 copy.20
  17.3 4.4 select_reduce_fusion
  21.8 30.5 %scatter_custom_fusion = s32[16384]{0:T(1024)S(1)} fusion(s32[8192]{0:T(1024)S(1)} %bitcast.86, s32[8192]{0:T(1024)S(1)} %iota.15, s32[]{:T(128)} %constant.117.clone.1), kind=kCustom, calls=%fused_computation.39 | custom fusion | bytes 65540 | tf_op jit(solution)/shard_map/scatter | solution.py:259
  52.4 0.7 fusion.7
  53.1 0.7 copy.18
  53.8 2.3 all-to-all-start
  56.6 0.6 fusion.13
  59.8 27.0 %gather_fusion = bf16[2048,2304]{1,0:T(8,128)(2,1)} fusion(bf16[4096,2304]{1,0:T(8,128)(2,1)} %refs_0_.5, s32[2048]{0:T(1024)S(1)} %broadcast_clamp_fusion.7), kind=kCustom, calls=%fused_computation | custom fusion | bytes 18882560 | tf_op jit(solution)/shard_map/gather | solution.py:275
  86.8 0.6 fusion.12
  90.0 0.6 pad_add_fusion.3.count_ref
  90.6 320.9 %all-to-all-done = s32[8,1,2176]{2,1,0:T(1,128)S(1)} async-done(((s32[8,1,2176]{2,1,0:T(1,128)}), s32[8,1,2176]{2,1,0:T(1,128)S(1)}, u32[]{:S(2)}, u32[]{:S(2)}) %all-to-all-start) | async-done | bytes 69664 | tf_op jit(solution)/shard_map/all_to_all | solution.py:264
  411.5 0.6 copy.23
  412.1 27.0 %gather_fusion.1 = bf16[2048,2304]{1,0:T(8,128)(2,1)} fusion(bf16[4096,2304]{1,0:T(8,128)(2,1)} %collective-permute-done.3, s32[2048]{0:T(1024)S(1)} %broadcast_clamp_fusion.6), kind=kCustom, calls=%fused_computation.1 | custom fusion | bytes 18882560 | tf_op jit(solution)/shard_map/gather | solution.py:275
  439.1 113.6 %shard_map.73 = (bf16[2048,2304]{1,0:T(8,128)(2,1)}, bf16[2048,2304]{1,0:T(8,128)(2,1)}) custom-call(s32[2]{0:T(128)} %pad_add_fusion.3.count_ref, bf16[2048,2304]{1,0:T(8,128)(2,1)} %gather_fusion, bf16[2048,2304]{1,0:T(8,128)(2,1)} %gather_fusion.1, bf16[2304,5760]{1,0:T(8,128)(2,1)} %bitcast.104, bf16[5760,2304]{1,0:T(8,128)(2,1)} %bitcast.109), custom_call_target="tpu_custom_call" | custom-call | flops 108716359680 | bytes 90832896 | tf_op jit(solution)/shard_map/pallas_call | solution.py:105
  552.8 112.8 %shard_map.74.refs_1_ = bf16[1536,2304]{1,0:T(8,128)(2,1)} custom-call(s32[1]{0:T(128)} %constant.121.clone.1.count_ref, bf16[4096,2304]{1,0:T(8,128)(2,1)} %refs_0_.5, bf16[2304,5760]{1,0:T(8,128)(2,1)} %refs_1_.3, bf16[5760,2304]{1,0:T(8,128)(2,1)} %refs_2_.3), custom_call_target="tpu_custom_call" | custom-call | flops 40768634880 | bytes 67239936 | tf_op jit(solution)/shard_map/pallas_call | solution.py:105
  666.2 7.8 slice.134
  674.0 7.9 slice.135
  681.9 0.6 gather_fusion.5
  683.3 0.6 gather_fusion.4
  684.0 0.7 fusion.9
  684.6 3.2 pad_add_fusion.6
  687.8 0.7 compare_select_fusion.1
  688.5 27.0 %gather_fusion.6 = bf16[2048,2304]{1,0:T(8,128)(2,1)} fusion(bf16[4096,2304]{1,0:T(8,128)(2,1)} %collective-permute-done, s32[2048]{0:T(1024)S(1)} %broadcast_clamp_fusion.5), kind=kCustom, calls=%fused_computation.6 | custom fusion | bytes 18882560 | tf_op jit(solution)/shard_map/gather | solution.py:275
  715.5 27.0 %gather_fusion.7 = bf16[2048,2304]{1,0:T(8,128)(2,1)} fusion(bf16[4096,2304]{1,0:T(8,128)(2,1)} %collective-permute-done.1, s32[2048]{0:T(1024)S(1)} %broadcast_clamp_fusion.4), kind=kCustom, calls=%fused_computation.7 | custom fusion | bytes 18882560 | tf_op jit(solution)/shard_map/gather | solution.py:275
  742.6 48.7 %collective-permute-start.7 = (bf16[2048,2304]{1,0:T(8,128)(2,1)}, bf16[2048,2304]{1,0:T(8,128)(2,1)}, u32[]{:S(2)}, u32[]{:S(2)}) collective-permute-start(bf16[2048,2304]{1,0:T(8,128)(2,1)} %slice.135), channel_id=1, source_target_pairs={{0,2},{1,3},{2,0},{3,1},{4,6},{5,7},{6,4},{7,5}} | collective-permute-start | bytes 28311560 | tf_op jit(solution)/shard_map/ppermute | solution.py:241
  791.3 97.3 %collective-permute-start.6 = (bf16[2048,2304]{1,0:T(8,128)(2,1)}, bf16[2048,2304]{1,0:T(8,128)(2,1)}, u32[]{:S(2)}, u32[]{:S(2)}) collective-permute-start(bf16[2048,2304]{1,0:T(8,128)(2,1)} %slice.134), channel_id=1, source_target_pairs={{0,4},{1,5},{2,6},{3,7},{4,0},{5,1},{6,2},{7,3}} | collective-permute-start | bytes 28311560 | tf_op jit(solution)/shard_map/ppermute | solution.py:241
  888.7 129.5 %shard_map.75 = (bf16[2048,2304]{1,0:T(8,128)(2,1)}, bf16[2048,2304]{1,0:T(8,128)(2,1)}) custom-call(s32[2]{0:T(128)} %get-tuple-element.27.count_ref, bf16[2048,2304]{1,0:T(8,128)(2,1)} %gather_fusion.6, bf16[2048,2304]{1,0:T(8,128)(2,1)} %gather_fusion.7, bf16[2304,5760]{1,0:T(8,128)(2,1)} %bitcast.105, bf16[5760,2304]{1,0:T(8,128)(2,1)} %bitcast.110), custom_call_target="tpu_custom_call" | custom-call | flops 108716359680 | bytes 90832896 | tf_op jit(solution)/shard_map/pallas_call | solution.py:105
  1018.2 73.6 %collective-permute-done.6 = bf16[2048,2304]{1,0:T(8,128)(2,1)} collective-permute-done((bf16[2048,2304]{1,0:T(8,128)(2,1)}, bf16[2048,2304]{1,0:T(8,128)(2,1)}, u32[]{:S(2)}, u32[]{:S(2)}) %collective-permute-start.6) | collective-permute-done | bytes 9437216 | tf_op jit(solution)/shard_map/ppermute | solution.py:241
  1091.8 8.0 constant_dynamic-update-slice_fusion.1
  1099.9 8.1 constant_dynamic-update-slice_fusion
  1108.0 0.7 gather_fusion.3
  1108.7 0.6 copy.19
  1109.3 1.8 reshape.413.gate_ref
  1111.2 0.6 pad_add_fusion.2.pair_ref
  1111.8 0.6 pad_add_fusion.1.pair_ref
  1113.0 0.7 fusion.5
  1113.6 0.8 gather_fusion.2
  1114.4 0.7 fusion.11
  1115.1 1.8 pad_add_fusion.4
  1116.9 0.6 broadcast_clamp_fusion
  1117.6 27.2 %gather_fusion.10 = bf16[2048,2304]{1,0:T(8,128)(2,1)} fusion(bf16[4096,2304]{1,0:T(8,128)(2,1)} %constant_dynamic-update-slice_fusion, s32[2048]{0:T(1024)S(1)} %broadcast_clamp_fusion.1), kind=kCustom, calls=%fused_computation.10 | custom fusion | bytes 18882560 | tf_op jit(solution)/shard_map/gather | solution.py:275
  1144.8 1.7 collective-permute-start.11
  1146.5 27.0 %gather_fusion.8 = bf16[2048,2304]{1,0:T(8,128)(2,1)} fusion(bf16[4096,2304]{1,0:T(8,128)(2,1)} %collective-permute-done.4, s32[2048]{0:T(1024)S(1)} %broadcast_clamp_fusion.3), kind=kCustom, calls=%fused_computation.8 | custom fusion | bytes 18882560 | tf_op jit(solution)/shard_map/gather | solution.py:275
  1173.6 27.0 %gather_fusion.9 = bf16[2048,2304]{1,0:T(8,128)(2,1)} fusion(bf16[4096,2304]{1,0:T(8,128)(2,1)} %collective-permute-done.5, s32[2048]{0:T(1024)S(1)} %broadcast_clamp_fusion.2), kind=kCustom, calls=%fused_computation.9 | custom fusion | bytes 18882560 | tf_op jit(solution)/shard_map/gather | solution.py:275
  1200.6 65.9 %shard_map.76 = (bf16[2048,2304]{1,0:T(8,128)(2,1)}, bf16[2048,2304]{1,0:T(8,128)(2,1)}) custom-call(s32[2]{0:T(128)} %get-tuple-element.31.count_ref, bf16[2048,2304]{1,0:T(8,128)(2,1)} %gather_fusion.8, bf16[2048,2304]{1,0:T(8,128)(2,1)} %gather_fusion.9, bf16[2304,5760]{1,0:T(8,128)(2,1)} %bitcast.106, bf16[5760,2304]{1,0:T(8,128)(2,1)} %bitcast.111), custom_call_target="tpu_custom_call" | custom-call | flops 108716359680 | bytes 90832896 | tf_op jit(solution)/shard_map/pallas_call | solution.py:105
  1266.5 81.7 %shard_map.77 = bf16[2048,2304]{1,0:T(8,128)(2,1)} custom-call(s32[1]{0:T(128)} %get-tuple-element.33.count_ref, bf16[2048,2304]{1,0:T(8,128)(2,1)} %gather_fusion.10, bf16[2304,5760]{1,0:T(8,128)(2,1)} %bitcast.107, bf16[5760,2304]{1,0:T(8,128)(2,1)} %bitcast.112), custom_call_target="tpu_custom_call" | custom-call | flops 54358179840 | bytes 71958528 | tf_op jit(solution)/shard_map/pallas_call | solution.py:105
  1348.2 208.1 %collective-permute-start.14 = (bf16[2048,2304]{1,0:T(8,128)(2,1)}, bf16[2048,2304]{1,0:T(8,128)(2,1)}, u32[]{:S(2)}, u32[]{:S(2)}) collective-permute-start(bf16[2048,2304]{1,0:T(8,128)(2,1)} %shard_map.77), channel_id=1, source_target_pairs={{0,6},{1,7},{2,4},{3,5},{4,2},{5,3},{6,0},{7,1}} | collective-permute-start | bytes 28311560 | tf_op jit(solution)/shard_map/ppermute | solution.py:241
  1556.3 27.1 %gather_fusion.11 = bf16[2048,2304]{1,0:T(8,128)(2,1)} fusion(bf16[4096,2304]{1,0:T(8,128)(2,1)} %collective-permute-done.8, s32[2048]{0:T(1024)} %broadcast_clamp_fusion), kind=kCustom, calls=%fused_computation.11 | custom fusion | bytes 18882560 | tf_op jit(solution)/shard_map/gather | solution.py:275
  1583.4 81.8 %shard_map.78 = bf16[2048,2304]{1,0:T(8,128)(2,1)} custom-call(s32[1]{0:T(128)} %get-tuple-element.36.count_ref, bf16[2048,2304]{1,0:T(8,128)(2,1)} %gather_fusion.11, bf16[2304,5760]{1,0:T(8,128)(2,1)} %bitcast.108, bf16[5760,2304]{1,0:T(8,128)(2,1)} %bitcast.113), custom_call_target="tpu_custom_call" | custom-call | flops 54358179840 | bytes 71958528 | tf_op jit(solution)/shard_map/pallas_call | solution.py:105
  1665.2 32.1 %collective-permute-start.13 = (bf16[2048,2304]{1,0:T(8,128)(2,1)}, bf16[2048,2304]{1,0:T(8,128)(2,1)}, u32[]{:S(2)}, u32[]{:S(2)}) collective-permute-start(bf16[2048,2304]{1,0:T(8,128)(2,1)} %get-tuple-element.40), channel_id=1, source_target_pairs={{0,5},{1,4},{2,7},{3,6},{4,1},{5,0},{6,3},{7,2}} | collective-permute-start | bytes 28311560 | tf_op jit(solution)/shard_map/ppermute | solution.py:241
  1697.3 176.4 %shard_map.79.refs_2_ = bf16[2560,2304]{1,0:T(8,128)(2,1)} custom-call(s32[1]{0:T(128)} %constant.130.clone.1.count_ref, bf16[4096,2304]{1,0:T(8,128)(2,1)} %refs_0_.5, bf16[2304,5760]{1,0:T(8,128)(2,1)} %refs_1_.3, bf16[5760,2304]{1,0:T(8,128)(2,1)} %refs_2_.3), custom_call_target="tpu_custom_call" | custom-call | flops 67947724800 | bytes 76677120 | tf_op jit(solution)/shard_map/pallas_call | solution.py:105
  1873.7 62.8 %shard_map.80.refs_0_ = f32[4096,2304]{1,0:T(8,128)} custom-call(s32[4]{0:T(128)} %get-tuple-element.68.count_ref, s32[8192]{0:T(1024)} %pad_add_fusion.2.pair_ref, f32[8192]{0:T(1024)} %reshape.413.gate_ref, bf16[4096,2304]{1,0:T(8,128)(2,1)} %refs_0_.5, bf16[1536,2304]{1,0:T(8,128)(2,1)} %shard_map.74.refs_1_, bf16[2560,2304]{1,0:T(8,128)(2,1)} %shard_map.79.refs_2_, ...), custom_call_target="tpu_custom_call" | custom-call | flops 60000002048 | bytes 56623104 | tf_op jit(solution)/shard_map/pallas_call | solution.py:220
  1936.5 166.7 %collective-permute-done.13.refs_2_ = bf16[2048,2304]{1,0:T(8,128)(2,1)} collective-permute-done((bf16[2048,2304]{1,0:T(8,128)(2,1)}, bf16[2048,2304]{1,0:T(8,128)(2,1)}, u32[]{:S(2)}, u32[]{:S(2)}) %collective-permute-start.13) | collective-permute-done | bytes 9437216 | tf_op jit(solution)/shard_map/ppermute | solution.py:241
  2103.2 88.1 %shard_map.81 = bf16[4096,2304]{1,0:T(8,128)(2,1)} custom-call(s32[4]{0:T(128)} %get-tuple-element.67.count_ref, s32[8192]{0:T(1024)} %pad_add_fusion.1.pair_ref, f32[8192]{0:T(1024)} %reshape.413.gate_ref, f32[4096,2304]{1,0:T(8,128)} %shard_map.80.refs_0_, bf16[2048,2304]{1,0:T(8,128)(2,1)} %collective-permute-done.12.refs_1_, ...), custom_call_target="tpu_custom_call" | custom-call | flops 60000002048 | bytes 56623104 | tf_op jit(solution)/shard_map/pallas_call | solution.py:220
  (73 shorter events, 3.5 us)
Async XLA Ops:
  0.0 412.1 %collective-permute-start.3 = (bf16[4096,2304]{1,0:T(8,128)(2,1)}, bf16[4096,2304]{1,0:T(8,128)(2,1)}, u32[]{:S(2)}, u32[]{:S(2)}) collective-permute-start(bf16[4096,2304]{1,0:T(8,128)(2,1)} %refs_0_.5), channel_id=1, source_target_pairs={{0,1},{1,0},{2,3},{3,2},{4,5},{5,4},{6,7},{7,6}} | collective-permute-start | bytes 56623112 | tf_op jit(solution)/shard_map/ppermute | solution.py:241
  0.8 664.8 %collective-permute-start.1 = (bf16[4096,2304]{1,0:T(8,128)(2,1)}, bf16[4096,2304]{1,0:T(8,128)(2,1)}, u32[]{:S(2)}, u32[]{:S(2)}) collective-permute-start(bf16[4096,2304]{1,0:T(8,128)(2,1)} %refs_0_.5), channel_id=1, source_target_pairs={{0,4},{1,5},{2,6},{3,7},{4,0},{5,1},{6,2},{7,3}} | collective-permute-start | bytes 56623112 | tf_op jit(solution)/shard_map/ppermute | solution.py:241
  3.3 662.3 %collective-permute-start = (bf16[4096,2304]{1,0:T(8,128)(2,1)}, bf16[4096,2304]{1,0:T(8,128)(2,1)}, u32[]{:S(2)}, u32[]{:S(2)}) collective-permute-start(bf16[4096,2304]{1,0:T(8,128)(2,1)} %refs_0_.5), channel_id=1, source_target_pairs={{0,2},{1,3},{2,0},{3,1},{4,6},{5,7},{6,4},{7,5}} | collective-permute-start | bytes 56623112 | tf_op jit(solution)/shard_map/ppermute | solution.py:241
  52.4 34.5 %copy-start = (s32[8,2048]{1,0:T(8,128)}, s32[8,2048]{1,0:T(8,128)S(1)}, u32[]{:S(2)}) copy-start(s32[8,2048]{1,0:T(8,128)S(1)} %reshape.412) | copy-start | bytes 196612
  53.8 357.7 %all-to-all-start = ((s32[8,1,2176]{2,1,0:T(1,128)}), s32[8,1,2176]{2,1,0:T(1,128)S(1)}, u32[]{:S(2)}, u32[]{:S(2)}) async-start(s32[8,1,2176]{2,1,0:T(1,128)} %copy.18), calls=%async_computation | async-start | bytes 139264 | tf_op jit(solution)/shard_map/all_to_all | solution.py:264
  56.1 30.7 %collective-permute-start.2 = (s32[1,2176]{1,0:T(1,128)S(1)}, s32[1,2176]{1,0:T(1,128)S(1)}, u32[]{:S(2)}, u32[]{:S(2)}) collective-permute-start(s32[1,2176]{1,0:T(1,128)S(1)} %constant_dynamic-slice_fusion.2), channel_id=1, source_target_pairs={{0,1},{1,0},{2,3},{3,2},{4,5},{5,4},{6,7},{7,6}} | collective-permute-start | bytes 26120 | tf_op jit(solution)/shard_map/ppermute | solution.py:241
  665.6 479.2 %collective-permute-start.4 = (bf16[4096,2304]{1,0:T(8,128)(2,1)}, bf16[4096,2304]{1,0:T(8,128)(2,1)}, u32[]{:S(2)}, u32[]{:S(2)}) collective-permute-start(bf16[4096,2304]{1,0:T(8,128)(2,1)} %collective-permute-done), channel_id=1, source_target_pairs={{0,1},{1,0},{2,3},{3,2},{4,5},{5,4},{6,7},{7,6}} | collective-permute-start | bytes 56623112 | tf_op jit(solution)/shard_map/ppermute | solution.py:241
  665.7 507.9 %collective-permute-start.5 = (bf16[4096,2304]{1,0:T(8,128)(2,1)}, bf16[4096,2304]{1,0:T(8,128)(2,1)}, u32[]{:S(2)}, u32[]{:S(2)}) collective-permute-start(bf16[4096,2304]{1,0:T(8,128)(2,1)} %collective-permute-done.1), channel_id=1, source_target_pairs={{0,1},{1,0},{2,3},{3,2},{4,5},{5,4},{6,7},{7,6}} | collective-permute-start | bytes 56623112 | tf_op jit(solution)/shard_map/ppermute | solution.py:241
  666.2 17.1 copy-start.9
  674.0 7.9 copy-start.2
  682.5 0.6 copy-start.8
  742.6 275.6 %collective-permute-start.7 = (bf16[2048,2304]{1,0:T(8,128)(2,1)}, bf16[2048,2304]{1,0:T(8,128)(2,1)}, u32[]{:S(2)}, u32[]{:S(2)}) collective-permute-start(bf16[2048,2304]{1,0:T(8,128)(2,1)} %slice.135), channel_id=1, source_target_pairs={{0,2},{1,3},{2,0},{3,1},{4,6},{5,7},{6,4},{7,5}} | collective-permute-start | bytes 28311560 | tf_op jit(solution)/shard_map/ppermute | solution.py:241
  791.3 300.5 %collective-permute-start.6 = (bf16[2048,2304]{1,0:T(8,128)(2,1)}, bf16[2048,2304]{1,0:T(8,128)(2,1)}, u32[]{:S(2)}, u32[]{:S(2)}) collective-permute-start(bf16[2048,2304]{1,0:T(8,128)(2,1)} %slice.134), channel_id=1, source_target_pairs={{0,4},{1,5},{2,6},{3,7},{4,0},{5,1},{6,2},{7,3}} | collective-permute-start | bytes 28311560 | tf_op jit(solution)/shard_map/ppermute | solution.py:241
  1099.8 8.1 copy-start.1
  1099.8 8.8 copy-start.3
  1099.8 17.1 copy-start.7
  1099.8 17.7 copy-start.6
  1099.8 17.7 copy-start.5
  1099.9 17.7 copy-start.4
  1108.0 448.3 %collective-permute-start.8 = (bf16[4096,2304]{1,0:T(8,128)(2,1)}, bf16[4096,2304]{1,0:T(8,128)(2,1)}, u32[]{:S(2)}, u32[]{:S(2)}) collective-permute-start(bf16[4096,2304]{1,0:T(8,128)(2,1)} %constant_dynamic-update-slice_fusion), channel_id=1, source_target_pairs={{0,1},{1,0},{2,3},{3,2},{4,5},{5,4},{6,7},{7,6}} | collective-permute-start | bytes 56623112 | tf_op jit(solution)/shard_map/ppermute | solution.py:241
  1112.5 761.3 %collective-permute-start.10 = (bf16[2048,2304]{1,0:T(8,128)(2,1)}, bf16[2048,2304]{1,0:T(8,128)(2,1)}, u32[]{:S(2)}, u32[]{:S(2)}) collective-permute-start(bf16[2048,2304]{1,0:T(8,128)(2,1)} %get-tuple-element.30), channel_id=1, source_target_pairs={{0,2},{1,3},{2,0},{3,1},{4,6},{5,7},{6,4},{7,5}} | collective-permute-start | bytes 28311560 | tf_op jit(solution)/shard_map/ppermute | solution.py:241
  1112.7 552.4 %collective-permute-start.9 = (bf16[2048,2304]{1,0:T(8,128)(2,1)}, bf16[2048,2304]{1,0:T(8,128)(2,1)}, u32[]{:S(2)}, u32[]{:S(2)}) collective-permute-start(bf16[2048,2304]{1,0:T(8,128)(2,1)} %get-tuple-element.38), channel_id=1, source_target_pairs={{0,1},{1,0},{2,3},{3,2},{4,5},{5,4},{6,7},{7,6}} | collective-permute-start | bytes 28311560 | tf_op jit(solution)/shard_map/ppermute | solution.py:241
  1144.8 552.5 %collective-permute-start.11 = (bf16[2048,2304]{1,0:T(8,128)(2,1)}, bf16[2048,2304]{1,0:T(8,128)(2,1)}, u32[]{:S(2)}, u32[]{:S(2)}) collective-permute-start(bf16[2048,2304]{1,0:T(8,128)(2,1)} %get-tuple-element.39), channel_id=1, source_target_pairs={{0,4},{1,5},{2,6},{3,7},{4,0},{5,1},{6,2},{7,3}} | collective-permute-start | bytes 28311560 | tf_op jit(solution)/shard_map/ppermute | solution.py:241
  1348.2 588.3 %collective-permute-start.14 = (bf16[2048,2304]{1,0:T(8,128)(2,1)}, bf16[2048,2304]{1,0:T(8,128)(2,1)}, u32[]{:S(2)}, u32[]{:S(2)}) collective-permute-start(bf16[2048,2304]{1,0:T(8,128)(2,1)} %shard_map.77), channel_id=1, source_target_pairs={{0,6},{1,7},{2,4},{3,5},{4,2},{5,3},{6,0},{7,1}} | collective-permute-start | bytes 28311560 | tf_op jit(solution)/shard_map/ppermute | solution.py:241
  1556.3 546.9 %collective-permute-start.12 = (bf16[2048,2304]{1,0:T(8,128)(2,1)}, bf16[2048,2304]{1,0:T(8,128)(2,1)}, u32[]{:S(2)}, u32[]{:S(2)}) collective-permute-start(bf16[2048,2304]{1,0:T(8,128)(2,1)} %get-tuple-element.32), channel_id=1, source_target_pairs={{0,3},{1,2},{2,1},{3,0},{4,7},{5,6},{6,5},{7,4}} | collective-permute-start | bytes 28311560 | tf_op jit(solution)/shard_map/ppermute | solution.py:241
  1665.2 438.0 %collective-permute-start.13 = (bf16[2048,2304]{1,0:T(8,128)(2,1)}, bf16[2048,2304]{1,0:T(8,128)(2,1)}, u32[]{:S(2)}, u32[]{:S(2)}) collective-permute-start(bf16[2048,2304]{1,0:T(8,128)(2,1)} %get-tuple-element.40), channel_id=1, source_target_pairs={{0,5},{1,4},{2,7},{3,6},{4,1},{5,0},{6,3},{7,2}} | collective-permute-start | bytes 28311560 | tf_op jit(solution)/shard_map/ppermute | solution.py:241
  1697.3 405.9 %collective-permute-start.15 = (bf16[2048,2304]{1,0:T(8,128)(2,1)}, bf16[2048,2304]{1,0:T(8,128)(2,1)}, u32[]{:S(2)}, u32[]{:S(2)}) collective-permute-start(bf16[2048,2304]{1,0:T(8,128)(2,1)} %shard_map.78), channel_id=1, source_target_pairs={{0,7},{1,6},{2,5},{3,4},{4,3},{5,2},{6,1},{7,0}} | collective-permute-start | bytes 28311560 | tf_op jit(solution)/shard_map/ppermute | solution.py:241
